TPU v7x, 8 devices: a whole 2x2x1 slice. The times are simulated.
8 devices in a mesh: sys: 1 (over z), aux: 2 (over y), orb: 4 (over x, core).
Axes of the slice: x: 2, y: 2, z: 1, core: 2. Of those that a mesh axis runs over, the one named last changes fastest.
Arguments:
- aux_ints: float32 [672, 192, 192], P(('sys', 'aux'), 'orb')
- metric: float32 [672, 672], P(('sys', 'aux'))
- orbitals: float32 [4, 192, 40], P('sys')
Outputs:
- output: float32 [4, 192, 192], P('sys', 'orb', 'aux')
All inputs are finite; a program needn't handle non-finite values.
Results may differ from a plain program's by a relative error of at most 0.001.
Values are sent between devices in bfloat16 or wider.
A program may use at most 1 GiB of HBM per device.

v0:
```python
import jax
import jax.numpy as jnp
from jax import lax
from jax.sharding import PartitionSpec as P

PRECISE = lax.Precision.HIGHEST


def solution(mesh):
    def local_fock(ints_blk, metric_blk, orbitals):
        m_loc = ints_blk.shape[1]
        row_start = lax.axis_index('orb') * m_loc
        half_tr = jnp.einsum('qml,dli->qmdi', ints_blk, orbitals, precision=PRECISE, preferred_element_type=jnp.float32)
        orb_rows = lax.dynamic_slice_in_dim(orbitals, row_start, m_loc, axis=1)
        gamma_part = jnp.einsum('qmdi,dmi->dq', half_tr, orb_rows, precision=PRECISE, preferred_element_type=jnp.float32)
        gamma_raw = lax.psum(gamma_part, 'orb')
        gamma_all = lax.all_gather(gamma_raw, 'aux', axis=1, tiled=True)
        gamma_fit = jnp.einsum('dq,pq->dp', gamma_all, metric_blk, precision=PRECISE, preferred_element_type=jnp.float32)
        weight_part = jnp.dot(gamma_fit, metric_blk, precision=PRECISE, preferred_element_type=jnp.float32)
        weights = lax.psum_scatter(weight_part, 'aux', scatter_dimension=1, tiled=True)
        coulomb = jnp.einsum('dq,qmn->dmn', weights, ints_blk, precision=PRECISE, preferred_element_type=jnp.float32)
        half_all = lax.all_gather(half_tr, 'aux', axis=0, tiled=True)
        fitted = jnp.einsum('pq,qmdi->pmdi', metric_blk, half_all, precision=PRECISE, preferred_element_type=jnp.float32)
        fitted_all = lax.all_gather(fitted, 'orb', axis=1, tiled=True)
        exchange = jnp.einsum('pmdi,pndi->dmn', fitted, fitted_all, precision=PRECISE, preferred_element_type=jnp.float32)
        fock_part = 2.0 * coulomb - exchange
        return lax.psum_scatter(fock_part, 'aux', scatter_dimension=2, tiled=True)

    return jax.shard_map(local_fock, mesh=mesh, in_specs=(P(('sys', 'aux'), 'orb', None), P(('sys', 'aux'), None), P('sys', None, None)), out_specs=P('sys', 'orb', 'aux'), check_vma=False)
```

profile of v0, /device:TPU:0, one launch (start us, length us, event | category | flops | bytes accessed | tf_op | source)
XLA Modules:
  0.0 1186.9 jit_solution(3316899028407229992)
XLA Ops:
  6.5 0.0 copy-start
  6.5 0.0 copy-start.1
  6.5 0.0 all-gather.4.cloned.1.call-start
  6.5 18.2 %copy.23 = f32[336,48,192,1]{2,1,3,0:T(8,128)} copy(f32[336,48,192,1]{0,2,1,3:T(8,128)} %bitcast.44) | data formatting | bytes 24772608 | tf_op args[0]
  24.7 0.0 copy-done.1
  24.7 29.6 %fusion.13 = f32[336,48,4,40]{1,3,2,0:T(8,128)} fusion(f32[336,48,192,1]{2,1,3,0:T(8,128)} %copy.23, f32[4,192,40]{1,2,0:T(8,128)S(1)} %copy-done.1), kind=kOutput, calls=%fused_computation.12 | convolution fusion | flops 5945425920 | bytes 22831104 | tf_op jit(solution)/shard_map/qml,dli->qmdi/dot_general | solution.py:13
  54.3 0.0 all-gather.4.cloned.1.call-update
  54.4 0.2 all-gather.6.cloned.1.call-start
  54.6 631.1 %all-gather.4.cloned.1.call-done = f32[672,48,4,40]{1,3,2,0:T(8,128)} async-done(((f32[336,48,4,40]{1,3,2,0:T(8,128)}), f32[672,48,4,40]{1,3,2,0:T(8,128)}) %all-gather.4.cloned.1.call-update) | async-done | bytes 20643856 | tf_op jit(solution)/shard_map/all_gather | solution.py:22
  685.7 49.0 %copy.18 = f32[672,48,4,40]{0,3,2,1:T(8,128)} copy(f32[672,48,4,40]{1,3,2,0:T(8,128)} %all-gather.4.cloned.1.call-done) | data formatting | bytes 41287680 | tf_op jit(solution)/shard_map/all_gather | solution.py:22
  734.8 0.0 copy-done
  734.8 40.9 %convolution_bitcast_fusion = f32[336,48,4,40]{0,3,2,1:T(8,128)} fusion(f32[672,48,4,40]{0,3,2,1:T(8,128)} %copy.18, f32[336,672]{1,0:T(8,128)S(1)} %copy-done), kind=kOutput, calls=%fused_computation.5 | convolution fusion | flops 20808990720 | bytes 31868928 | tf_op jit(solution)/shard_map/pq,qmdi->pmdi/dot_general | solution.py:23
  775.7 0.0 all-gather.6.cloned.1.call-update
  775.7 0.0 reduce-scatter.7.cloned.1.call-start
  775.8 0.1 constant_dynamic-slice_fusion
  775.9 28.4 %fusion.2 = f32[4,1,336,1]{2,1,3,0:T(1,128)S(1)} fusion(f32[4,48,40,1]{1,3,2,0:T(1,128)S(1)} %bitcast.47, f32[336,48,4,40]{1,3,2,0:T(8,128)} %fusion.13), kind=kOutput, calls=%fused_computation.2 | convolution fusion | flops 30965760 | bytes 10358016 | tf_op jit(solution)/shard_map/qmdi,dmi->dq/dot_general | solution.py:15
  804.3 7.2 psum.7
  811.5 4.3 all-gather
  815.9 0.1 reshape.1
  815.9 0.9 fusion.15
  816.8 2.8 convolution_bitcast_fusion.1
  819.6 0.0 reduce-scatter.7.cloned.1.call-update
  819.6 0.0 reduce-scatter.9.cloned.1.call-start
  819.7 233.5 %all-gather.6.cloned.1.call-done = f32[336,192,4,40]{0,3,2,1:T(8,128)} async-done(((f32[336,48,4,40]{0,3,2,1:T(8,128)}), f32[336,192,4,40]{0,3,2,1:T(8,128)}) %all-gather.6.cloned.1.call-update) | async-done | bytes 41287696 | tf_op jit(solution)/shard_map/all_gather | solution.py:24
  1053.2 89.4 %fusion.6 = f32[4,48,192]{2,1,0:T(8,128)S(1)} fusion(f32[336,192,4,40]{0,3,2,1:T(8,128)} %all-gather.6.cloned.1.call-done, f32[336,48,4,40]{0,3,2,1:T(8,128)} %convolution_bitcast_fusion), kind=kOutput, calls=%fused_computation.9 | convolution fusion | flops 5945425920 | bytes 51757056 | tf_op jit(solution)/shard_map/pmdi,pndi->dmn/dot_general | solution.py:25
  1142.6 0.0 reduce-scatter.7.cloned.1.call-done
  1142.6 18.0 %fusion.5 = f32[4,48,192]{2,0,1:T(4,128)S(1)} fusion(f32[336,48,192]{0,2,1:T(8,128)} %param.3, f32[4,48,192]{2,1,0:T(8,128)S(1)} %fusion.6, f32[336,4]{1,0:T(8,128)} %reduce-scatter.7.cloned.1.call-done), kind=kOutput, calls=%fused_computation.8 | convolution fusion | flops 148709376 | bytes 12686592 | tf_op jit(solution)/shard_map/dq,qmn->dmn/dot_general | solution.py:21
  1160.6 3.1 copy.33
  1163.7 4.4 reshape.11
  1168.1 0.0 reduce-scatter.9.cloned.1.call-update
  1168.1 8.3 reduce-scatter.9.cloned.1.call-done
  1176.4 2.2 reshape.12
  1178.6 1.5 copy.22
  (2 shorter events, 0.0 us)
Async XLA Ops:
  6.5 728.2 %copy-start = (f32[336,672]{1,0:T(8,128)S(1)}, f32[336,672]{1,0:T(8,128)}, u32[]{:S(2)}) copy-start(f32[336,672]{1,0:T(8,128)} %param.4) | copy-start | bytes 2709508
  6.5 18.2 %copy-start.1 = (f32[4,192,40]{1,2,0:T(8,128)S(1)}, f32[4,192,40]{1,2,0:T(8,128)}, u32[]{:S(2)}) copy-start(f32[4,192,40]{1,2,0:T(8,128)} %param.5) | copy-start | bytes 368644
  6.5 679.2 %all-gather.4.cloned.1.call-start = ((), (), s32[]{:S(2)}) async-start(), calls=%async_computation.2 | async-start | bytes 82575360 | tf_op jit(solution)/shard_map/all_gather | solution.py:22
  54.4 998.8 %all-gather.6.cloned.1.call-start = ((), (), s32[]{:S(2)}) async-start(), calls=%async_computation.3 | async-start | bytes 58982400 | tf_op jit(solution)/shard_map/all_gather | solution.py:24
  775.7 366.8 %reduce-scatter.7.cloned.1.call-start = ((), (), s32[]{:S(2)}) async-start(), calls=%async_computation.4 | async-start | bytes 516096
  819.6 356.8 %reduce-scatter.9.cloned.1.call-start = ((), (), s32[]{:S(2)}) async-start(), calls=%async_computation.5 | async-start | bytes 294912
Sparse Core Ops, SparseCore 0:
  54.5 631.1 all-gather.3
  775.9 277.2 all-gather.5
  1055.4 9.7 reduce-scatter.6
  1168.2 8.1 reduce-scatter.8
where the time goes:
time: 1190 us
  waiting for transfers between devices  873 us (73%)
  matrix products  210 us (18%)
  local copies, waits for them, and re-layouts  78.6 us (7%)
  between operations  13.4 us (1%)
    all_gather x1, waiting for transfers between devices, local_fock(): half_all = lax.all_gather(half_tr, 'aux', axis=0, tiled=True)  631 us
    all_gather x1, waiting for transfers between devices, local_fock(): fitted_all = lax.all_gather(fitted, 'orb', axis=1, tiled=True)  233 us
    dot_general x1, matrix products, local_fock(): jnp.einsum('pmdi,pndi->dmn', fitted, fitted_all, precision=PRECISE, prefe...  89.4 us
    all_gather x1, local copies, waits for them, and re-layouts, local_fock(): half_all = lax.all_gather(half_tr, 'aux', axis=0, tiled=True)  49 us
    dot_general x1, matrix products, local_fock(): jnp.einsum('pq,qmdi->pmdi', metric_blk, half_all, precision=PRECISE, pref...  40.9 us
    dot_general x1, matrix products, local_fock(): jnp.einsum('qml,dli->qmdi', ints_blk, orbitals, precision=PRECISE, prefer...  29.6 us
    dot_general x1, matrix products, local_fock(): jnp.einsum('qmdi,dmi->dq', half_tr, orb_rows, precision=PRECISE, preferre...  28.4 us
    unnamed x9, local copies, waits for them, and re-layouts  27.9 us
  transfers between devices with their start and end apart: 4, of which 3 were waited for; matrix products, arithmetic and copies ran while one was open for 10% of the time, Pallas kernels for 0%

commit v1 on v0

v1 whole, which is shorter than its diff:
```python
import functools

import jax
import jax.numpy as jnp
from jax import lax
from jax.experimental import pallas as pl
from jax.experimental.pallas import tpu as pltpu
from jax.sharding import PartitionSpec as P

MESH = pl.DeviceIdType.MESH
F32, BF16 = jnp.float32, jnp.bfloat16
HIGHEST = lax.Precision.HIGHEST

DENS, L, OCC = 4, 192, 40
COLS = DENS * OCC
MINE = COLS // 8
ROWS = 48
GROUP = 16
GROUPS = ROWS // GROUP
QL, QP = 336, 384
TAIL = QL - 256
STRIDE = 168
NT = (((1,), (1,)), ((), ()))


def _subsets(sizes):
    out, first, off = [], 0, 0
    for n in sizes:
        tails = 2 * (n // 3) + n % 3
        out.append((first, n, off, 2 * n + tails))
        first, off = first + n, off + 2 * n + tails
    return out, off


SUBSETS, SLOTS = _subsets((8, 8, 4))
MAXSUB = max(s[1] for s in SUBSETS)


def _split(v):
    one = v.astype(BF16)
    rest = v - one.astype(F32)
    two = rest.astype(BF16)
    return one, two, (rest - two.astype(F32)).astype(BF16)


def _dot(p, q):
    return jnp.dot(p, q, preferred_element_type=F32)


def _dot_nt(p, q):
    return lax.dot_general(p, q, NT, preferred_element_type=F32)


def _padq(v):
    return jnp.pad(v, ((0, 0), (0, QP - QL)))


def kernel(b_hbm, ct_ref, met_ref, out_ref,
           b_ref, c_ref, dfull, dm_ref, s_ref, snd, rcv, hl, m_ref, mx, mr, t_ref,
           ga_ref, gr_ref, j_ref, jown, jsend, jrecv, kacc, xacc, ksend, krecv,
           bsem, hs_sem, hr_sem, ms_sem, mr_sem, gs_sem, gr_sem, js_sem, jr_sem, ks_sem, kr_sem):
    a = lax.axis_index('aux')
    o = lax.axis_index('orb')
    x, c = o // 2, o % 2
    sys = lax.axis_index('sys')

    def peer(k):
        return (a + k // 4) % 2, (x + (k // 2) % 2) % 2, (c + k % 2) % 2

    def device(k):
        pa, px, pc = peer(k)
        return (sys, pa, px * 2 + pc)

    def remote(src, dst, ssem, rsem, k):
        return pltpu.make_async_remote_copy(src_ref=src, dst_ref=dst, send_sem=ssem, recv_sem=rsem,
                                            device_id=device(k), device_id_type=MESH)

    def b_copy(g):
        return pltpu.make_async_copy(b_hbm.at[pl.ds(g * GROUP, GROUP)], b_ref.at[pl.ds(g * GROUP, GROUP)], bsem.at[g])

    def h_copy(k, g, s):
        _, _, off, n = SUBSETS[s]
        return remote(snd.at[k - 1, g, pl.ds(off, n)], rcv.at[k, g, pl.ds(off, n)],
                      hs_sem.at[k, g, s], hr_sem.at[k, g, s], k)

    ORDER = (2, 4, 6, 3, 5, 7, 1)

    def h_send(g, s):
        for k in ORDER:
            h_copy(k, g, s).start()

    def m_copy(step):
        rows = pl.ds(pl.multiple_of(c * (QL // 2), 8), QL // 2)
        return remote((mx if step == 0 else mr).at[rows], mr.at[rows], ms_sem.at[step], mr_sem.at[step], 4 if step == 0 else 1)

    def g_copy(k):
        return remote(ga_ref, gr_ref.at[k], gs_sem.at[k], gr_sem.at[k], k)

    def j_copy():
        return remote(jsend, jrecv, js_sem, jr_sem, 4)

    def k_copy(k):
        return remote(ksend.at[k], krecv.at[k], ks_sem.at[k], kr_sem.at[k], k)

    for g in range(GROUPS):
        b_copy(g).start()

    barrier = pltpu.get_barrier_semaphore()
    for k in range(1, 8):
        pl.semaphore_signal(barrier, inc=1, device_id=device(k), device_id_type=MESH)

    met = met_ref[...]
    low, high = _padq(met[:, :QL]), _padq(met[:, QL:])
    own = jnp.where(a == 0, low, high)
    oth = jnp.where(a == 0, high, low)
    mx[...] = own

    def m_store(block, row, col):
        for j, term in enumerate(_split(block)):
            m_ref[pl.ds(j * 2 * QP + row, block.shape[0]), pl.ds(col, QP)] = term

    m_store(oth, 0, QP)
    m_store(jnp.pad(oth, ((0, QP - QL), (0, 0))).T, QP, 0)
    m_store(own, 0, 0)
    for j in range(3):
        m_ref[pl.ds(j * 2 * QP + QL, QP - QL), :] = jnp.zeros((QP - QL, 2 * QP), BF16)
        m_ref[pl.ds(j * 2 * QP + QP + QL, QP - QL), pl.ds(QP, QP)] = jnp.zeros((QP - QL, QP), BF16)
    pl.semaphore_wait(barrier, 7)
    m_copy(0).start()

    for j, term in enumerate(_split(ct_ref[...])):
        c_ref[j] = term
    dm_ref[...] = jnp.zeros_like(dm_ref)
    for d in range(DENS):
        cd = ct_ref[pl.ds(d * OCC, OCC), :]
        dfull[...] = lax.dot_general(cd, cd, (((0,), (0,)), ((), ())), precision=HIGHEST, preferred_element_type=F32)
        dm_ref[:, d, :] = dfull[pl.ds(pl.multiple_of(o * ROWS, 8), ROWS), :]

    lane = lax.broadcasted_iota(jnp.int32, (GROUP, 128), 1)

    def half_transform(g):
        def body(p, ga):
            m = g * GROUP + 2 * p
            b1, b2, b3 = _split(jnp.concatenate([_padq(b_ref[m]), _padq(b_ref[m + 1])], axis=1))
            d1, d2, d3 = _split(dm_ref[pl.ds(m, 2)].reshape(16, L))
            lhs = jnp.concatenate([c_ref[0], d1, c_ref[1], d2, c_ref[2], d3], axis=0)
            n = COLS + 16
            r1, r2, r3 = _dot(lhs, b1), _dot(lhs[:2 * n], b2), _dot(lhs[:n], b3)
            h = r1[:n] + ((r1[n:2 * n] + r2[:n]) + (r1[2 * n:] + (r2[n:] + r3)))
            for q in range(2):
                for t in range(3):
                    s_ref[t, pl.ds(pl.multiple_of((2 * p + q) * STRIDE, 8), COLS), :] = h[:COLS, q * QP + t * 128:q * QP + (t + 1) * 128]
            return ga + h[COLS:COLS + 8, :QP] + h[COLS + 8:, QP:]

        ga_ref[...] = lax.fori_loop(0, GROUP // 2, body, jnp.zeros((8, QP), F32) if g == 0 else ga_ref[...])

    def pack(k, g, dst):
        pa, px, pc = peer(k)
        first = (pa * 4 + px * 2 + pc) * MINE

        def load(t, i):
            return s_ref[t, pl.ds(first + i, GROUP, stride=STRIDE), :]

        for i0, n, off, _ in SUBSETS:
            for i in range(n):
                dst[off + i] = load(0, i0 + i).astype(BF16)
                dst[off + n + i] = load(1, i0 + i).astype(BF16)
            at = off + 2 * n
            for j in range(n // 3):
                third = load(2, i0 + 3 * j + 2)
                dst[at + 2 * j] = jnp.where(lane < TAIL, load(2, i0 + 3 * j), pltpu.roll(third, TAIL, 1)).astype(BF16)
                dst[at + 2 * j + 1] = jnp.where(lane < TAIL, load(2, i0 + 3 * j + 1), pltpu.roll(third, 32, 1)).astype(BF16)
            for i in range(n - n % 3, n):
                dst[at + 2 * (n // 3) + i - (n - n % 3)] = load(2, i0 + i).astype(BF16)

    def pack_all(g):
        def body(k, carry):
            pack(k, g, snd.at[k - 1, g])
            return carry

        lax.fori_loop(1, 8, body, 0)
        pack(0, g, rcv.at[0, g])
        first = (a * 4 + x * 2 + c) * MINE
        for i in range(MINE):
            for t in range(3):
                _, two, three = _split(s_ref[t, pl.ds(first + i, GROUP, stride=STRIDE), :])
                hl[0, g, i, :, pl.ds(t * 128, 128)] = two
                hl[1, g, i, :, pl.ds(t * 128, 128)] = three

    b_copy(0).wait()
    half_transform(0)
    pack_all(0)
    h_send(0, 0)
    b_copy(1).wait()
    half_transform(1)
    pack_all(1)
    m_copy(0).wait_recv()
    m_copy(1).start()
    b_copy(2).wait()
    half_transform(2)
    for k in (1, 2, 3, 4, 5, 6, 7):
        g_copy(k).start()
    h_send(1, 0)
    pack_all(2)
    h_send(2, 0)
    for g in range(GROUPS):
        h_send(g, 1)

    m_copy(1).wait_recv()
    m_store(mr[...], QP, QP)

    for k in range(1, 8):
        g_copy(k).wait_recv()
    gam = jnp.concatenate([ga_ref[...] + gr_ref[1] + gr_ref[2] + gr_ref[3],
                           gr_ref[4] + gr_ref[5] + gr_ref[6] + gr_ref[7]], axis=1)

    def stack(v):
        return jnp.concatenate([t.astype(F32) for t in _split(v)], axis=0).astype(BF16)

    def three(v, dot):
        r1, r2, r3 = dot(v, 0), dot(v[:16], 1), dot(v[:8], 2)
        return r1[:8] + ((r1[8:16] + r2[:8]) + (r1[16:] + (r2[8:] + r3)))

    fit = three(stack(gam), lambda v, j: _dot(v, m_ref[pl.ds(j * 2 * QP, 2 * QP), :]))
    weights = three(stack(fit), lambda v, j: _dot(v, m_ref[pl.ds(j * 2 * QP, 2 * QP), pl.ds(0, QP)]))
    wstack = stack(weights)

    def coulomb(m, carry):
        terms = _split(_padq(b_ref[m]))
        j_ref[m] = three(wstack, lambda v, j: _dot_nt(v, terms[j]))
        return carry

    lax.fori_loop(0, ROWS, coulomb, 0)
    for d in range(DENS):
        jd = j_ref[:, d, :]
        jown[d] = jnp.where(a == 0, jd[:, :96], jd[:, 96:])
        jsend[d] = jnp.where(a == 0, jd[:, 96:], jd[:, :96])
    j_copy().start()

    kacc[...] = jnp.zeros_like(kacc)
    xacc[...] = jnp.zeros_like(xacc)

    for s, (i0, n, off, _) in enumerate(SUBSETS):
        if s == 1:
            for g in range(GROUPS):
                h_send(g, 2)

        def half(k, g):
            first = rcv[k, g, pl.ds(off, n)].reshape(n * GROUP, 128)
            second = rcv[k, g, pl.ds(off + n, n)].reshape(n * GROUP, 128)
            at, tails = off + 2 * n, []
            for j in range(n // 3):
                p, q = rcv[k, g, at + 2 * j], rcv[k, g, at + 2 * j + 1]
                third = jnp.where(lane < 128 - TAIL, pltpu.roll(p.astype(F32), 128 - TAIL, 1), pltpu.roll(q.astype(F32), 96, 1))
                tails += [p, q, third.astype(BF16)]
            for i in range(n % 3):
                tails.append(rcv[k, g, at + 2 * (n // 3) + i])
            return jnp.concatenate([first, second, jnp.concatenate(tails, axis=0)], axis=1)

        def fit_group(g, carry):
            for k in range(1, 8):
                h_copy(k, g, s).wait_recv()
            lhs = jnp.concatenate([jnp.concatenate([half(k, g), half(k + 4, g)], axis=1) for k in range(4)], axis=0)
            t = _dot(jnp.concatenate([lhs, lhs, lhs], axis=1), m_ref[...])
            h2 = hl[0, g, pl.ds(i0, n)].reshape(n * GROUP, QP)
            h3 = hl[1, g, pl.ds(i0, n)].reshape(n * GROUP, QP)
            ca = _dot(jnp.concatenate([h2, h3], axis=0), m_ref[pl.ds(0, QP), :])
            cb = _dot(h2, m_ref[pl.ds(2 * QP, QP), :])
            w = n * GROUP
            for k in range(4):
                _, px, pc = peer(k)
                part = t[k * w:(k + 1) * w]
                if k == 0:
                    part = part + (ca[:w] + (ca[w:] + cb))
                row = pl.multiple_of((px * 2 + pc) * ROWS + g * GROUP, GROUP)
                t_ref[pl.ds(0, n), pl.ds(row, GROUP), :] = part.reshape(n, GROUP, 2 * QP)
            return carry

        lax.fori_loop(0, GROUPS, fit_group, 0)

        def exchange(i, carry):
            t1, t2, t3 = _split(t_ref[i])
            one = jnp.concatenate([t1, t2], axis=1)
            kacc[...] += _dot_nt(one, one)
            xacc[...] += _dot_nt(jnp.concatenate([t1, t1], axis=1), jnp.concatenate([t2, t3], axis=1))
            return carry

        lax.fori_loop(0, n, exchange, 0)

    kacc[...] += xacc[...] + xacc[...].T
    for k in (7, 6, 5, 4, 3, 2, 1, 0):
        pa, px, pc = peer(k)
        rows = kacc[pl.ds(pl.multiple_of((px * 2 + pc) * ROWS, 8), ROWS), :]
        part = jnp.where(pa == 0, rows[:, :96], rows[:, 96:])
        if k:
            ksend[k] = part
        else:
            krecv[0] = part
    for k in (7, 6, 5, 4, 3, 2, 1):
        k_copy(k).start()
    j_copy().wait_recv()
    for k in range(1, 8):
        k_copy(k).wait_recv()
    for k in (0, 2, 4, 6):
        pa, px, _ = peer(k)
        d = pa * 2 + px
        out_ref[d] = 2.0 * (jown[d] + jrecv[d]) - (krecv[k] + krecv[k + 1])

    for k in range(1, 8):
        for g in range(GROUPS):
            for s in range(len(SUBSETS)):
                h_copy(k, g, s).wait_send()
        g_copy(k).wait_send()
        k_copy(k).wait_send()
    m_copy(0).wait_send()
    m_copy(1).wait_send()
    j_copy().wait_send()


def solution(mesh):
    def local_fock(ints_blk, metric_blk, orbitals):
        bt = jnp.transpose(ints_blk, (1, 2, 0))
        ct = jnp.transpose(orbitals, (0, 2, 1)).reshape(COLS, L)
        ns = len(SUBSETS)
        dma = pltpu.SemaphoreType.DMA
        return pl.pallas_call(
            kernel,
            out_shape=jax.ShapeDtypeStruct((DENS, ROWS, 96), F32),
            in_specs=[pl.BlockSpec(memory_space=pl.ANY), pl.BlockSpec(memory_space=pltpu.VMEM), pl.BlockSpec(memory_space=pltpu.VMEM)],
            out_specs=pl.BlockSpec(memory_space=pltpu.VMEM),
            scratch_shapes=[
                pltpu.VMEM((ROWS, L, QL), F32),
                pltpu.VMEM((3, COLS, L), BF16),
                pltpu.VMEM((L, L), F32),
                pltpu.VMEM((ROWS, 8, L), F32),
                pltpu.VMEM((3, GROUP * STRIDE, 128), F32),
                pltpu.VMEM((7, GROUPS, SLOTS, GROUP, 128), BF16),
                pltpu.VMEM((8, GROUPS, SLOTS, GROUP, 128), BF16),
                pltpu.VMEM((2, GROUPS, MINE, GROUP, QP), BF16),
                pltpu.VMEM((6 * QP, 2 * QP), BF16),
                pltpu.VMEM((QL, QP), F32),
                pltpu.VMEM((QL, QP), F32),
                pltpu.VMEM((MAXSUB, L, 2 * QP), F32),
                pltpu.VMEM((8, QP), F32),
                pltpu.VMEM((8, 8, QP), F32),
                pltpu.VMEM((ROWS, 8, L), F32),
                pltpu.VMEM((DENS, ROWS, 96), F32),
                pltpu.VMEM((DENS, ROWS, 96), F32),
                pltpu.VMEM((DENS, ROWS, 96), F32),
                pltpu.VMEM((L, L), F32),
                pltpu.VMEM((L, L), F32),
                pltpu.VMEM((8, ROWS, 96), F32),
                pltpu.VMEM((8, ROWS, 96), F32),
                dma((GROUPS,)), dma((8, GROUPS, ns)), dma((8, GROUPS, ns)), dma((2,)), dma((2,)),
                dma((8,)), dma((8,)), dma, dma, dma((8,)), dma((8,)),
            ],
            compiler_params=pltpu.CompilerParams(collective_id=0, has_side_effects=True, vmem_limit_bytes=60 * 1024 * 1024),
            cost_estimate=pl.CostEstimate(flops=25_000_000_000, bytes_accessed=16_000_000, transcendentals=0),
        )(bt, ct, metric_blk)

    return jax.shard_map(local_fock, mesh=mesh, in_specs=(P(('sys', 'aux'), 'orb', None), P(('sys', 'aux'), None), P('sys', None, None)), out_specs=P('sys', 'orb', 'aux'), check_vma=False)
```

time: 1190 us -> 89.5 us (0.08)
  waiting for transfers between devices: 873 us -> 0 us
  matrix products: 210 us -> 0 us
  Pallas kernels: 0 us -> 87.8 us
  local copies, waits for them, and re-layouts: 78.6 us -> 1.54 us
  between operations: 13.4 us -> 0.01 us
    all_gather x2 -> x0, waiting for transfers between devices: 865 us -> none  [the longest x1 631 us: local_fock(): half_all = lax.all_gather(half_tr, 'aux', axis=0, tiled=True)]
    dot_general x6 -> x0, matrix products: 207 us -> none  [the longest x1 89.4 us: local_fock(): jnp.einsum('pmdi,pndi->dmn', fitted, fitted_all, precision=PRECISE, prefe...]
    pallas_call x0 -> x1, Pallas kernels: none -> 87.8 us  [local_fock(): pl.pallas_call(kernel, out_shape=jax.ShapeDtypeStruct((DENS, ROWS, 96), F...]
    all_gather x2 -> x0, local copies, waits for them, and re-layouts: 49 us -> none  [the longest x1 49 us: local_fock(): half_all = lax.all_gather(half_tr, 'aux', axis=0, tiled=True)]
    unnamed x9 -> x1, local copies, waits for them, and re-layouts: 27.9 us -> 1.54 us
  transfers between devices with their start and end apart: 4 -> 0, of which waited for: 3 -> 0; matrix products, arithmetic and copies ran while one was open for 10% -> 0% of each run, Pallas kernels for 0% -> 0%
where the time goes in v1:
time: 89.5 us; the launch traced here: 89.4 us
  Pallas kernels  87.8 us (98%)
  local copies, waits for them, and re-layouts  1.54 us (2%)
    pallas_call x1, Pallas kernels, local_fock(): pl.pallas_call(kernel, out_shape=jax.ShapeDtypeStruct((DENS, ROWS, 96), F...  87.8 us

profile of v1, /device:TPU:0, one launch (start us, length us, event | category | flops | bytes accessed | tf_op | source)
XLA Modules:
  0.0 89.4 jit_solution(14608698156466620791)
XLA Ops:
  0.0 87.8 %shard_map.37 = f32[4,48,96]{2,1,0:T(8,128)} custom-call(f32[48,192,336]{2,1,0:T(8,128)} %bitcast.4, f32[160,192]{1,0:T(8,128)} %bitcast.5, f32[336,672]{1,0:T(8,128)} %met_ref.1), custom_call_target="tpu_custom_call" | custom-call | flops 24999999488 | bytes 16000000 | tf_op jit(solution)/shard_map/pallas_call | solution.py:326
  87.8 1.5 %copy.5 = f32[4,48,96]{2,1,0:T(8,128)} copy(f32[4,48,96]{2,1,0:T(8,128)} %shard_map.37) | data formatting | bytes 147456

commit v2 on v1

--- a/solution.py
+++ b/solution.py
@@ -20,6 +20,9 @@
 QL, QP = 336, 384
 TAIL = QL - 256
 STRIDE = 168
+HALFC = COLS // 2
+MQ = 88
+WPAD = 32
 NT = (((1,), (1,)), ((), ()))
 
 
@@ -32,7 +35,7 @@
     return out, off
 
 
-SUBSETS, SLOTS = _subsets((8, 8, 4))
+SUBSETS, SLOTS = _subsets((9, 6, 3, 2))
 MAXSUB = max(s[1] for s in SUBSETS)
 
 
@@ -55,10 +58,10 @@
     return jnp.pad(v, ((0, 0), (0, QP - QL)))
 
 
-def kernel(b_hbm, ct_ref, met_ref, out_ref,
-           b_ref, c_ref, dfull, dm_ref, s_ref, snd, rcv, hl, m_ref, mx, mr, t_ref,
+def kernel(b_hbm, ct_hbm, met_hbm, out_ref,
+           b_ref, ct_ref, met_ref, c_ref, ctt, dm_ref, s_ref, snd, rcv, hl, m_ref, mx, mr, t_ref, w_ref,
            ga_ref, gr_ref, j_ref, jown, jsend, jrecv, kacc, xacc, ksend, krecv,
-           bsem, hs_sem, hr_sem, ms_sem, mr_sem, gs_sem, gr_sem, js_sem, jr_sem, ks_sem, kr_sem):
+           bsem, isem, hs_sem, hr_sem, ms_sem, mr_sem, gs_sem, gr_sem, js_sem, jr_sem, ks_sem, kr_sem):
     a = lax.axis_index('aux')
     o = lax.axis_index('orb')
     x, c = o // 2, o % 2
@@ -75,23 +78,24 @@
         return pltpu.make_async_remote_copy(src_ref=src, dst_ref=dst, send_sem=ssem, recv_sem=rsem,
                                             device_id=device(k), device_id_type=MESH)
 
-    def b_copy(g):
-        return pltpu.make_async_copy(b_hbm.at[pl.ds(g * GROUP, GROUP)], b_ref.at[pl.ds(g * GROUP, GROUP)], bsem.at[g])
+    def b_copy(j):
+        return pltpu.make_async_copy(b_hbm.at[pl.ds(j * 8, 8)], b_ref.at[pl.ds(j * 8, 8)], bsem.at[j])
 
     def h_copy(k, g, s):
         _, _, off, n = SUBSETS[s]
         return remote(snd.at[k - 1, g, pl.ds(off, n)], rcv.at[k, g, pl.ds(off, n)],
                       hs_sem.at[k, g, s], hr_sem.at[k, g, s], k)
 
-    ORDER = (2, 4, 6, 3, 5, 7, 1)
-
-    def h_send(g, s):
-        for k in ORDER:
+    FAR, NEAR = (4, 6, 5, 7), (2, 3, 1)
+
+    def h_send(g, s, ks=(4, 6, 2, 5, 7, 3, 1)):
+        for k in ks:
             h_copy(k, g, s).start()
 
     def m_copy(step):
-        rows = pl.ds(pl.multiple_of(c * (QL // 2), 8), QL // 2)
-        return remote((mx if step == 0 else mr).at[rows], mr.at[rows], ms_sem.at[step], mr_sem.at[step], 4 if step == 0 else 1)
+        mine = o if step < 3 else (1 - x) * 2 + c
+        src = mx.at[pl.ds(pl.multiple_of(o * MQ - (o // 3) * (4 * MQ - QL), 8), MQ)] if step == 0 else mr.at[mine]
+        return remote(src, mr.at[mine], ms_sem.at[step], mr_sem.at[step], (4, 2, 1, 1)[step])
 
     def g_copy(k):
         return remote(ga_ref, gr_ref.at[k], gs_sem.at[k], gr_sem.at[k], k)
@@ -102,57 +106,75 @@
     def k_copy(k):
         return remote(ksend.at[k], krecv.at[k], ks_sem.at[k], kr_sem.at[k], k)
 
-    for g in range(GROUPS):
-        b_copy(g).start()
+    ct_copy = pltpu.make_async_copy(ct_hbm, ct_ref, isem.at[0])
+    met_copy = pltpu.make_async_copy(met_hbm, met_ref, isem.at[1])
+    ct_copy.start()
+    met_copy.start()
+    for j in range(ROWS // 8):
+        b_copy(j).start()
 
     barrier = pltpu.get_barrier_semaphore()
     for k in range(1, 8):
         pl.semaphore_signal(barrier, inc=1, device_id=device(k), device_id_type=MESH)
 
+    ct_copy.wait()
+    for j, term in enumerate(_split(ct_ref[...])):
+        c_ref[j] = term
+
+    met_copy.wait()
     met = met_ref[...]
     low, high = _padq(met[:, :QL]), _padq(met[:, QL:])
     own = jnp.where(a == 0, low, high)
-    oth = jnp.where(a == 0, high, low)
     mx[...] = own
+    pl.semaphore_wait(barrier, 7)
 
     def m_store(block, row, col):
         for j, term in enumerate(_split(block)):
             m_ref[pl.ds(j * 2 * QP + row, block.shape[0]), pl.ds(col, QP)] = term
 
-    m_store(oth, 0, QP)
-    m_store(jnp.pad(oth, ((0, QP - QL), (0, 0))).T, QP, 0)
-    m_store(own, 0, 0)
-    for j in range(3):
-        m_ref[pl.ds(j * 2 * QP + QL, QP - QL), :] = jnp.zeros((QP - QL, 2 * QP), BF16)
-        m_ref[pl.ds(j * 2 * QP + QP + QL, QP - QL), pl.ds(QP, QP)] = jnp.zeros((QP - QL, QP), BF16)
-    pl.semaphore_wait(barrier, 7)
-    m_copy(0).start()
-
-    for j, term in enumerate(_split(ct_ref[...])):
-        c_ref[j] = term
-    dm_ref[...] = jnp.zeros_like(dm_ref)
-    for d in range(DENS):
-        cd = ct_ref[pl.ds(d * OCC, OCC), :]
-        dfull[...] = lax.dot_general(cd, cd, (((0,), (0,)), ((), ())), precision=HIGHEST, preferred_element_type=F32)
-        dm_ref[:, d, :] = dfull[pl.ds(pl.multiple_of(o * ROWS, 8), ROWS), :]
-
     lane = lax.broadcasted_iota(jnp.int32, (GROUP, 128), 1)
 
-    def half_transform(g):
+    def density_rows():
+        ctt[...] = ct_ref[...].T
+        rows = ctt[pl.ds(pl.multiple_of(o * ROWS, 8), ROWS), :]
+        col = lax.broadcasted_iota(jnp.int32, (ROWS, COLS), 1)
+        masked = [jnp.where((col >= d * OCC) & (col < (d + 1) * OCC), rows, 0.0) for d in range(DENS)]
+        dens = jnp.dot(jnp.concatenate(masked, axis=0), ct_ref[...], precision=HIGHEST, preferred_element_type=F32)
+        dm_ref[...] = jnp.zeros_like(dm_ref)
+        for d in range(DENS):
+            dm_ref[:, d, :] = dens[d * ROWS:(d + 1) * ROWS]
+
+    def half_transform(g, start, n, with_gamma):
         def body(p, ga):
             m = g * GROUP + 2 * p
             b1, b2, b3 = _split(jnp.concatenate([_padq(b_ref[m]), _padq(b_ref[m + 1])], axis=1))
-            d1, d2, d3 = _split(dm_ref[pl.ds(m, 2)].reshape(16, L))
-            lhs = jnp.concatenate([c_ref[0], d1, c_ref[1], d2, c_ref[2], d3], axis=0)
-            n = COLS + 16
-            r1, r2, r3 = _dot(lhs, b1), _dot(lhs[:2 * n], b2), _dot(lhs[:n], b3)
-            h = r1[:n] + ((r1[n:2 * n] + r2[:n]) + (r1[2 * n:] + (r2[n:] + r3)))
+            terms = [c_ref[j, pl.ds(start, n), :] for j in range(3)]
+            if with_gamma:
+                extra = _split(dm_ref[pl.ds(m, 2)].reshape(16, L))
+                terms = [jnp.concatenate(pair, axis=0) for pair in zip(terms, extra)]
+            w = terms[0].shape[0]
+            lhs = jnp.concatenate(terms, axis=0)
+            r1, r2, r3 = _dot(lhs, b1), _dot(lhs[:2 * w], b2), _dot(lhs[:w], b3)
+            h = r1[:w] + ((r1[w:2 * w] + r2[:w]) + (r1[2 * w:] + (r2[w:] + r3)))
             for q in range(2):
+                row = pl.multiple_of((2 * p + q) * STRIDE + start, 8)
                 for t in range(3):
-                    s_ref[t, pl.ds(pl.multiple_of((2 * p + q) * STRIDE, 8), COLS), :] = h[:COLS, q * QP + t * 128:q * QP + (t + 1) * 128]
-            return ga + h[COLS:COLS + 8, :QP] + h[COLS + 8:, QP:]
-
-        ga_ref[...] = lax.fori_loop(0, GROUP // 2, body, jnp.zeros((8, QP), F32) if g == 0 else ga_ref[...])
+                    s_ref[t, pl.ds(row, n), :] = h[:n, q * QP + t * 128:q * QP + (t + 1) * 128]
+            if with_gamma:
+                ga = ga + h[n:n + 8, :QP] + h[n + 8:, QP:]
+            return ga
+
+        return body
+
+    def run_half(g, start, n, with_gamma, waits):
+        body = half_transform(g, start, n, with_gamma)
+        ga = (jnp.zeros((8, QP), F32) if g == 0 else ga_ref[...]) if with_gamma else 0
+        for j in range(2):
+            if waits:
+                b_copy(2 * g + j).wait()
+            ga = lax.fori_loop(4 * j, 4 * j + 4, body, ga)
+        if with_gamma:
+            ga_ref[...] = ga
 
     def pack(k, g, dst):
         pa, px, pc = peer(k)
@@ -173,12 +195,14 @@
             for i in range(n - n % 3, n):
                 dst[at + 2 * (n // 3) + i - (n - n % 3)] = load(2, i0 + i).astype(BF16)
 
-    def pack_all(g):
+    def pack_range(g, k0, k1):
         def body(k, carry):
             pack(k, g, snd.at[k - 1, g])
             return carry
 
-        lax.fori_loop(1, 8, body, 0)
+        lax.fori_loop(k0, k1, body, 0)
+
+    def pack_self(g):
         pack(0, g, rcv.at[0, g])
         first = (a * 4 + x * 2 + c) * MINE
         for i in range(MINE):
@@ -187,27 +211,50 @@
                 hl[0, g, i, :, pl.ds(t * 128, 128)] = two
                 hl[1, g, i, :, pl.ds(t * 128, 128)] = three
 
-    b_copy(0).wait()
-    half_transform(0)
-    pack_all(0)
-    h_send(0, 0)
-    b_copy(1).wait()
-    half_transform(1)
-    pack_all(1)
+    m_copy(0).start()
+    run_half(0, pl.multiple_of((1 - a) * HALFC, 16), HALFC, False, True)
+    pack_range(0, 4, 8)
+    h_send(0, 0, FAR)
+    h_send(0, 1, FAR)
     m_copy(0).wait_recv()
     m_copy(1).start()
-    b_copy(2).wait()
-    half_transform(2)
-    for k in (1, 2, 3, 4, 5, 6, 7):
+    m_copy(2).start()
+    density_rows()
+    run_half(0, pl.multiple_of(a * HALFC, 16), HALFC, True, False)
+    pack_range(0, 1, 4)
+    h_send(0, 0, NEAR)
+    h_send(0, 1, NEAR)
+    pack_self(0)
+    run_half(1, 0, COLS, True, True)
+    pack_range(1, 1, 8)
+    pack_self(1)
+    m_copy(1).wait_recv()
+    m_copy(3).start()
+    run_half(2, 0, COLS, True, True)
+    for k in (4, 6, 2, 5, 7, 3, 1):
         g_copy(k).start()
-    h_send(1, 0)
-    pack_all(2)
-    h_send(2, 0)
-    for g in range(GROUPS):
-        h_send(g, 1)
-
-    m_copy(1).wait_recv()
-    m_store(mr[...], QP, QP)
+    for s in (0, 1):
+        h_send(1, s)
+    pack_range(2, 1, 8)
+    for s in (0, 1):
+        h_send(2, s)
+    pack_self(2)
+
+    met = met_ref[...]
+    low, high = _padq(met[:, :QL]), _padq(met[:, QL:])
+    own = jnp.where(a == 0, low, high)
+    oth = jnp.where(a == 0, high, low)
+    m_store(own, 0, 0)
+    m_store(oth, 0, QP)
+    m_store(jnp.pad(oth, ((0, QP - QL), (0, 0))).T, QP, 0)
+    m_copy(2).wait_recv()
+    m_copy(3).wait_recv()
+    for q in range(3):
+        m_store(mr[q], QP + q * MQ, QP)
+    m_store(mr[3][4 * MQ - QL:], QP + 3 * MQ, QP)
+    for j in range(3):
+        m_ref[pl.ds(j * 2 * QP + QL, QP - QL), :] = jnp.zeros((QP - QL, 2 * QP), BF16)
+        m_ref[pl.ds(j * 2 * QP + QP + QL, QP - QL), pl.ds(QP, QP)] = jnp.zeros((QP - QL, QP), BF16)
 
     for k in range(1, 8):
         g_copy(k).wait_recv()
@@ -223,14 +270,22 @@
 
     fit = three(stack(gam), lambda v, j: _dot(v, m_ref[pl.ds(j * 2 * QP, 2 * QP), :]))
     weights = three(stack(fit), lambda v, j: _dot(v, m_ref[pl.ds(j * 2 * QP, 2 * QP), pl.ds(0, QP)]))
-    wstack = stack(weights)
-
-    def coulomb(m, carry):
-        terms = _split(_padq(b_ref[m]))
-        j_ref[m] = three(wstack, lambda v, j: _dot_nt(v, terms[j]))
+    wf = jnp.concatenate([t.astype(F32) for t in _split(weights)], axis=0)
+    for q in range(4):
+        blocks = [jnp.zeros((WPAD * q, QP), F32)] if q else []
+        wide = jnp.concatenate(blocks + [wf, jnp.zeros((128 - 24 - WPAD * q, QP), F32)], axis=0)
+        wt = wide.T.astype(BF16)
+        for j in range(3):
+            w_ref[pl.ds((3 * q + j) * QP, QP), :] = wt
+
+    def coulomb(p, carry):
+        terms = [t for q in range(4) for t in _split(_padq(b_ref[4 * p + q]))]
+        r = _dot(jnp.concatenate(terms, axis=1), w_ref[...]).T
+        for q in range(4):
+            j_ref[4 * p + q] = r[WPAD * q:WPAD * q + 8] + (r[WPAD * q + 8:WPAD * q + 16] + r[WPAD * q + 16:WPAD * q + 24])
         return carry
 
-    lax.fori_loop(0, ROWS, coulomb, 0)
+    lax.fori_loop(0, ROWS // 4, coulomb, 0)
     for d in range(DENS):
         jd = j_ref[:, d, :]
         jown[d] = jnp.where(a == 0, jd[:, :96], jd[:, 96:])
@@ -241,9 +296,12 @@
     xacc[...] = jnp.zeros_like(xacc)
 
     for s, (i0, n, off, _) in enumerate(SUBSETS):
+        if s == 0:
+            for g in range(GROUPS):
+                h_send(g, 2)
         if s == 1:
             for g in range(GROUPS):
-                h_send(g, 2)
+                h_send(g, 3)
 
         def half(k, g):
             first = rcv[k, g, pl.ds(off, n)].reshape(n * GROUP, 128)
@@ -280,9 +338,9 @@
 
         def exchange(i, carry):
             t1, t2, t3 = _split(t_ref[i])
-            one = jnp.concatenate([t1, t2], axis=1)
-            kacc[...] += _dot_nt(one, one)
-            xacc[...] += _dot_nt(jnp.concatenate([t1, t1], axis=1), jnp.concatenate([t2, t3], axis=1))
+            both = _dot_nt(jnp.concatenate([t1, t2], axis=0), t2)
+            kacc[...] += _dot_nt(t1, t1) + both[L:]
+            xacc[...] += both[:L] + _dot_nt(t1, t3)
             return carry
 
         lax.fori_loop(0, n, exchange, 0)
@@ -312,8 +370,8 @@
                 h_copy(k, g, s).wait_send()
         g_copy(k).wait_send()
         k_copy(k).wait_send()
-    m_copy(0).wait_send()
-    m_copy(1).wait_send()
+    for step in range(4):
+        m_copy(step).wait_send()
     j_copy().wait_send()
 
 
@@ -326,12 +384,14 @@
         return pl.pallas_call(
             kernel,
             out_shape=jax.ShapeDtypeStruct((DENS, ROWS, 96), F32),
-            in_specs=[pl.BlockSpec(memory_space=pl.ANY), pl.BlockSpec(memory_space=pltpu.VMEM), pl.BlockSpec(memory_space=pltpu.VMEM)],
+            in_specs=[pl.BlockSpec(memory_space=pltpu.HBM)] * 3,
             out_specs=pl.BlockSpec(memory_space=pltpu.VMEM),
             scratch_shapes=[
                 pltpu.VMEM((ROWS, L, QL), F32),
+                pltpu.VMEM((COLS, L), F32),
+                pltpu.VMEM((QL, 2 * QL), F32),
                 pltpu.VMEM((3, COLS, L), BF16),
-                pltpu.VMEM((L, L), F32),
+                pltpu.VMEM((L, COLS), F32),
                 pltpu.VMEM((ROWS, 8, L), F32),
                 pltpu.VMEM((3, GROUP * STRIDE, 128), F32),
                 pltpu.VMEM((7, GROUPS, SLOTS, GROUP, 128), BF16),
@@ -339,8 +399,9 @@
                 pltpu.VMEM((2, GROUPS, MINE, GROUP, QP), BF16),
                 pltpu.VMEM((6 * QP, 2 * QP), BF16),
                 pltpu.VMEM((QL, QP), F32),
-                pltpu.VMEM((QL, QP), F32),
+                pltpu.VMEM((4, MQ, QP), F32),
                 pltpu.VMEM((MAXSUB, L, 2 * QP), F32),
+                pltpu.VMEM((12 * QP, 128), BF16),
                 pltpu.VMEM((8, QP), F32),
                 pltpu.VMEM((8, 8, QP), F32),
                 pltpu.VMEM((ROWS, 8, L), F32),
@@ -351,10 +412,10 @@
                 pltpu.VMEM((L, L), F32),
                 pltpu.VMEM((8, ROWS, 96), F32),
                 pltpu.VMEM((8, ROWS, 96), F32),
-                dma((GROUPS,)), dma((8, GROUPS, ns)), dma((8, GROUPS, ns)), dma((2,)), dma((2,)),
+                dma((ROWS // 8,)), dma((2,)), dma((8, GROUPS, ns)), dma((8, GROUPS, ns)), dma((4,)), dma((4,)),
                 dma((8,)), dma((8,)), dma, dma, dma((8,)), dma((8,)),
             ],
-            compiler_params=pltpu.CompilerParams(collective_id=0, has_side_effects=True, vmem_limit_bytes=60 * 1024 * 1024),
+            compiler_params=pltpu.CompilerParams(collective_id=0, has_side_effects=True, vmem_limit_bytes=50 * 2**20),
             cost_estimate=pl.CostEstimate(flops=25_000_000_000, bytes_accessed=16_000_000, transcendentals=0),
         )(bt, ct, metric_blk)
 

time: 89.5 us -> 84.8 us (0.947)
  Pallas kernels: 87.8 us -> 81.9 us
  local copies, waits for them, and re-layouts: 1.54 us -> 2.78 us
    pallas_call x1, Pallas kernels: 87.8 us -> 81.9 us  [local_fock(): pl.pallas_call(kernel, out_shape=jax.ShapeDtypeStruct((DENS, ROWS, 96), F...]
    unnamed x1 -> x5, local copies, waits for them, and re-layouts: 1.54 us -> 2.78 us
where the time goes in v2:
time: 84.8 us; the launch traced here: 84.6 us
  Pallas kernels  81.9 us (97%)
  local copies, waits for them, and re-layouts  2.78 us (3%)
    pallas_call x1, Pallas kernels, local_fock(): pl.pallas_call(kernel, out_shape=jax.ShapeDtypeStruct((DENS, ROWS, 96), F...  81.9 us
    unnamed x5, local copies, waits for them, and re-layouts  2.78 us

profile of v2, /device:TPU:0, one launch (start us, length us, event | category | flops | bytes accessed | tf_op | source)
XLA Modules:
  0.0 84.6 jit_solution(9048848442063809394)
XLA Ops:
  0.0 0.0 copy-start
  0.0 1.2 %copy-done = f32[336,672]{1,0:T(8,128)S(1)} copy-done((f32[336,672]{1,0:T(8,128)S(1)}, f32[336,672]{1,0:T(8,128)}, u32[]{:S(2)}) %copy-start) | copy-done | bytes 903192
  1.2 0.0 copy-start.1
  1.2 0.9 %copy-done.1 = f32[4,192,40]{1,2,0:T(8,128)S(1)} copy-done((f32[4,192,40]{1,2,0:T(8,128)S(1)}, f32[4,192,40]{1,2,0:T(8,128)}, u32[]{:S(2)}) %copy-start.1) | copy-done | bytes 122904
  2.1 81.9 %shard_map.37 = f32[4,48,96]{2,1,0:T(8,128)S(1)} custom-call(f32[48,192,336]{2,1,0:T(8,128)} %bitcast.5, f32[160,192]{1,0:T(8,128)S(1)} %bitcast.4, f32[336,672]{1,0:T(8,128)S(1)} %copy-done), custom_call_target="tpu_custom_call" | custom-call | flops 24999999488 | bytes 16000000 | tf_op jit(solution)/shard_map/pallas_call | solution.py:384
  84.0 0.6 copy.5
Async XLA Ops:
  0.0 1.2 %copy-start = (f32[336,672]{1,0:T(8,128)S(1)}, f32[336,672]{1,0:T(8,128)}, u32[]{:S(2)}) copy-start(f32[336,672]{1,0:T(8,128)} %met_hbm.1) | copy-start | bytes 2709508
  1.2 0.9 %copy-start.1 = (f32[4,192,40]{1,2,0:T(8,128)S(1)}, f32[4,192,40]{1,2,0:T(8,128)}, u32[]{:S(2)}) copy-start(f32[4,192,40]{1,2,0:T(8,128)} %param.5) | copy-start | bytes 368644
